TPU v7x, 512 devices: a whole 4x4x16 slice. The times are simulated.
512 devices in a mesh: row: 16 (over z_hi, y), col: 4 (over x), cuts: 8 (over z_lo, core).
Axes of the slice: x: 4, y: 4, z: 16 (z_hi: 4, z_lo: 4; z = z_hi * 4 + z_lo), core: 2. Of those that a mesh axis runs over, the one named last changes fastest.
Arguments:
- warm: float32 [40, 131072], P('cuts', ('row', 'col')), may hold values from -6 to 6
- tiles: float32 [22016, 128, 128], P(('row', 'col', 'cuts')), may hold values from -0.125 to 0.125
- tile_rows: int32 [22016], P(('row', 'col', 'cuts')), may hold values from -1 to 1023, as said below
- tile_cols: int32 [22016], P(('row', 'col', 'cuts')), may hold values from 0 to 1023, as said below
Outputs:
- basis: float32 [40, 131072], P('cuts', ('row', 'col'))
- residual: float32 [40, 131072], P('cuts', ('row', 'col'))
Inputs may be any that keep to these rules, and one draw needn't show every extreme that they name: `tile_rows`: slots come in groups of 344; group r * (size of col) + c belongs to the grid position with row index r and column index c. A group's tiles lie in the block rows r * (size of col) * 16 up to (r + 1) * (size of col) * 16 - 1, and in block columns j with (j // 16) % (size of col) = c. No block appears twice. In each group the live slots come first and fill at least half of it; some group is full. Block rows hold uneven numbers of tiles. `tile_cols`: see tile_rows; an empty slot's column is that of some block the group may hold.
All inputs are finite; a program needn't handle non-finite values.
Results may differ from a plain program's by a relative error of at most 0.0003.
Values sent between devices are 32-bit elements; how exact they have to be, the bound alone decides.
A program may use at most 64 MiB of HBM per device.

v0:
```python
import jax
import jax.numpy as jnp
from jax import lax
from jax.sharding import PartitionSpec as P


def copy_for_each(shard, axis):
    devices = lax.axis_size(axis)
    return lax.all_to_all(
        jnp.broadcast_to(shard[None], (devices, *shard.shape)), axis, 0, 0, tiled=True
    )


def in_order(parts, dim):
    dims = list(parts.shape[1:])
    dims[dim] *= parts.shape[0]
    return jnp.moveaxis(parts, 0, dim).reshape(dims)


def collect(shard, axis, dim):
    parts = copy_for_each(shard, axis)
    return in_order(parts, dim)


def in_blocks(shard, dim, devices):
    dims = shard.shape
    parts = shard.reshape(*dims[:dim], devices, dims[dim] // devices, *dims[dim + 1 :])
    return jnp.moveaxis(parts, dim, 0)


def summed_on_arrival(shard, axis, dim):
    parts = in_blocks(shard, dim, lax.axis_size(axis))
    arrived = lax.all_to_all(parts, axis, split_axis=0, concat_axis=0, tiled=True)
    return arrived.sum(axis=0)


def over_copies(shard, axis):
    everything = copy_for_each(shard, axis)
    return jnp.sum(everything, axis=0)


def block_product(panel, tiles, rows, positions, base, out_blocks):
    count_rows = panel.shape[0]
    block = tiles.shape[1]
    blocks = panel.reshape(count_rows, -1, block)
    picked = jnp.take(blocks, positions, axis=1)
    prods = jnp.einsum("suv,ksv->ksu", tiles, picked, precision=lax.Precision.HIGHEST)
    local = rows - base
    onehot = (local[:, None] == jnp.arange(out_blocks, dtype=jnp.int32)[None, :]).astype(
        jnp.float32
    )
    summed = jnp.einsum("ksu,sb->kbu", prods, onehot, precision=lax.Precision.HIGHEST)
    return summed.reshape(count_rows, out_blocks * block)


def operator_apply(vectors, tiles, rows, positions, base, out_blocks):
    panel = collect(vectors, "cuts", 0)
    panel = lax.all_gather(panel, "row", axis=1, tiled=True)
    partial_value = block_product(panel, tiles, rows, positions, base, out_blocks)
    partial_value = summed_on_arrival(partial_value, "col", 1)
    return summed_on_arrival(partial_value, "cuts", 0)


def shards(warm, tiles, tile_rows, tile_cols):
    ncol = lax.axis_size("col")
    nrow = lax.axis_size("row")
    block = tiles.shape[1]
    seg_blocks = warm.shape[1] // block
    out_blocks = ncol * seg_blocks
    items = warm.shape[1] * nrow * ncol
    base = lax.axis_index("row") * out_blocks
    segment = tile_cols // seg_blocks
    positions = segment // ncol * seg_blocks + tile_cols % seg_blocks
    image = operator_apply(warm, tiles, tile_rows, positions, base, out_blocks)
    whole = collect(image, "cuts", 0)
    local_gram = jnp.dot(
        whole, whole.T, precision=lax.Precision.HIGHEST, preferred_element_type=jnp.float32
    )
    gram = over_copies(local_gram, ("row", "col")) / items
    lower = jnp.linalg.cholesky(gram)
    kloc = warm.shape[0]
    start = lax.axis_index("cuts") * kloc
    inverse = lax.linalg.triangular_solve(
        lower, jnp.eye(whole.shape[0], dtype=jnp.float32), left_side=True, lower=True
    )
    mine_rows = lax.dynamic_slice_in_dim(inverse, start, kloc, 0)
    basis = jnp.dot(
        mine_rows, whole, precision=lax.Precision.HIGHEST, preferred_element_type=jnp.float32
    )
    basis_all = collect(basis, "cuts", 0)
    product = operator_apply(basis, tiles, tile_rows, positions, base, out_blocks)
    local_projection = jnp.dot(
        basis_all, product.T, precision=lax.Precision.HIGHEST, preferred_element_type=jnp.float32
    )
    projected = over_copies(local_projection, ("row", "col")) / items
    residual = product - jnp.dot(
        projected.T, basis_all, precision=lax.Precision.HIGHEST, preferred_element_type=jnp.float32
    )
    return (basis, residual)


def solution(mesh):
    return jax.shard_map(
        shards,
        mesh=mesh,
        in_specs=(
            P("cuts", ("row", "col")),
            P(("row", "col", "cuts"), None, None),
            P(("row", "col", "cuts")),
            P(("row", "col", "cuts")),
        ),
        out_specs=(P("cuts", ("row", "col")), P("cuts", ("row", "col"))),
        check_vma=False,
    )
```

profile of v0, /device:TPU:1, one launch (start us, length us, event | category | flops | bytes accessed | tf_op | source)
XLA Modules:
  0.0 604.3 jit_solution(9353652540865754813)
XLA Ops:
  8.3 23.5 %all_to_all.46 = f32[8,5,2048]{2,1,0:T(8,128)S(1)} all-to-all(f32[8,5,2048]{2,1,0:T(8,128)S(1)} %broadcast_in_dim.20), channel_id=1, replica_groups=mesh['row'=16,'col'=4,'cuts'=8] {'cuts'}, dimensions={0} | all-to-all | bytes 655360 | tf_op jit(solution)/shard_map/all_to_all | solution.py:9
  32.7 155.9 %all-gather.3.cloned.1.call-done = f32[40,32768]{1,0:T(8,128)} async-done(((f32[40,2048]{1,0:T(8,128)}), f32[40,32768]{1,0:T(8,128)}) %all-gather.3.cloned.1.call-update) | async-done | bytes 5242896 | tf_op jit(solution)/shard_map/all_gather | solution.py:58
  188.6 5.2 copy_bitcast_fusion.1
  193.8 4.0 gather_fusion
  197.8 6.9 %convolution_bitcast_fusion.3 = f32[40,43,128]{2,0,1:T(8,128)S(1)} fusion(f32[43,128,128]{2,1,0:T(8,128)S(1)} %copy-done, f32[43,40,128]{2,1,0:T(8,128)} %gather_fusion, pred[43]{0:T(512)(128)(4,1)S(1)} %get-tuple-element.3), kind=kOutput, calls=%fused_computation.8 | convolution fusion | flops 338385920 | bytes 4579371 | tf_op jit(solution)/shard_map/suv,ksv->ksu/dot_general | solution.py:47
  204.6 1.9 convolution_bitcast_fusion.1
  206.5 2.7 reshape_reshape.6
  209.2 2.1 copy.55
  211.2 20.7 %all_to_all.47 = f32[4,40,2048]{2,1,0:T(8,128)} all-to-all(f32[4,40,2048]{2,1,0:T(8,128)S(1)} %bitcast.55), channel_id=1, replica_groups=mesh['row'=16,'col'=4,'cuts'=8] {'col'}, dimensions={0} | all-to-all | bytes 2621440 | tf_op jit(solution)/shard_map/all_to_all | solution.py:33
  232.0 2.2 reduce_sum.56
  235.1 19.3 %all_to_all.48 = f32[8,5,2048]{2,1,0:T(8,128)} all-to-all(f32[8,5,2048]{2,1,0:T(8,128)S(1)} %reshape.48), channel_id=1, replica_groups=mesh['row'=16,'col'=4,'cuts'=8] {'cuts'}, dimensions={0} | all-to-all | bytes 655360 | tf_op jit(solution)/shard_map/all_to_all | solution.py:33
  255.6 18.4 %all_to_all.49 = f32[8,5,2048]{2,1,0:T(8,128)} all-to-all(f32[8,5,2048]{2,1,0:T(8,128)S(1)} %broadcast_in_dim.22), channel_id=1, replica_groups=mesh['row'=16,'col'=4,'cuts'=8] {'cuts'}, dimensions={0} | all-to-all | bytes 655360 | tf_op jit(solution)/shard_map/all_to_all | solution.py:9
  276.6 3.2 reshape.76
  279.8 10.5 %all-to-all-start.4 = ((f32[64,1,1600]{2,1,0:T(1,128)}), f32[64,1,1600]{2,1,0:T(1,128)}, u32[]{:S(2)}, u32[]{:S(2)}) async-start(f32[64,1,1600]{2,1,0:T(1,128)} %reshape.76), calls=%async_computation.4 | async-start | bytes 851968 | tf_op jit(solution)/shard_map/all_to_all | solution.py:9
  290.5 24.7 %all-to-all-done.4 = f32[64,1,1600]{2,1,0:T(1,128)} async-done(((f32[64,1,1600]{2,1,0:T(1,128)}), f32[64,1,1600]{2,1,0:T(1,128)}, u32[]{:S(2)}, u32[]{:S(2)}) %all-to-all-start.4) | async-done | bytes 409632 | tf_op jit(solution)/shard_map/all_to_all | solution.py:9
  315.8 3.4 reduce.6
  319.2 2.6 reshape.77
  321.8 1.4 reduce_sum.58
  323.3 3.6 cholesky.17
  328.3 3.1 custom-call.6
  331.9 22.3 %all_to_all.50 = f32[8,5,2048]{2,1,0:T(8,128)S(1)} all-to-all(f32[8,5,2048]{2,1,0:T(8,128)S(1)} %broadcast_in_dim.24), channel_id=1, replica_groups=mesh['row'=16,'col'=4,'cuts'=8] {'cuts'}, dimensions={0} | all-to-all | bytes 655360 | tf_op jit(solution)/shard_map/all_to_all | solution.py:9
  355.0 146.8 %all-gather.5.cloned.1.call-done = f32[40,32768]{1,0:T(8,128)} async-done(((f32[40,2048]{1,0:T(8,128)}), f32[40,32768]{1,0:T(8,128)}) %all-gather.5.cloned.1.call-update) | async-done | bytes 5242896 | tf_op jit(solution)/shard_map/all_gather | solution.py:58
  501.9 5.1 copy_bitcast_fusion
  507.0 4.0 gather_fusion.1
  511.0 6.9 %convolution_bitcast_fusion.2 = f32[40,43,128]{2,0,1:T(8,128)S(1)} fusion(f32[43,128,128]{2,1,0:T(8,128)S(1)} %copy-done, f32[43,40,128]{2,1,0:T(8,128)} %gather_fusion.1, pred[43]{0:T(512)(128)(4,1)S(1)} %get-tuple-element.3), kind=kOutput, calls=%fused_computation.7 | convolution fusion | flops 338385920 | bytes 4579371 | tf_op jit(solution)/shard_map/suv,ksv->ksu/dot_general | solution.py:47
  517.9 1.9 convolution_bitcast_fusion
  519.8 2.7 reshape_reshape.7
  522.4 2.1 copy.54
  524.5 20.8 %all_to_all.51 = f32[4,40,2048]{2,1,0:T(8,128)} all-to-all(f32[4,40,2048]{2,1,0:T(8,128)S(1)} %bitcast.56), channel_id=1, replica_groups=mesh['row'=16,'col'=4,'cuts'=8] {'col'}, dimensions={0} | all-to-all | bytes 2621440 | tf_op jit(solution)/shard_map/all_to_all | solution.py:33
  545.4 1.4 reduce_sum.60
  547.6 20.3 %all_to_all.52 = f32[8,5,2048]{2,1,0:T(8,128)} all-to-all(f32[8,5,2048]{2,1,0:T(8,128)} %reshape.52), channel_id=1, replica_groups=mesh['row'=16,'col'=4,'cuts'=8] {'cuts'}, dimensions={0} | all-to-all | bytes 655360 | tf_op jit(solution)/shard_map/all_to_all | solution.py:33
  569.6 26.0 %all_to_all.53 = f32[64,1,200]{2,1,0:T(1,128)S(1)} all-to-all(f32[64,1,200]{2,1,0:T(1,128)S(1)} %reshape.78), channel_id=1, replica_groups=mesh['row'=16,'col'=4,'cuts'=8] {'row','col'}, dimensions={0} | all-to-all | bytes 102400 | tf_op jit(solution)/shard_map/all_to_all | solution.py:9
  (44 shorter events, 14.6 us)
Async XLA Ops:
  7.2 190.6 %copy-start = (f32[43,128,128]{2,1,0:T(8,128)S(1)}, f32[43,128,128]{2,1,0:T(8,128)}, u32[]{:S(2)}) copy-start(f32[43,128,128]{2,1,0:T(8,128)} %param.7) | copy-start | bytes 8454148
  7.2 25.4 %copy-start.3 = (s32[43]{0:T(128)S(1)}, s32[43]{0:T(128)}, u32[]{:S(2)}) copy-start(s32[43]{0:T(128)} %param.9) | copy-start | bytes 520
  7.2 25.5 %copy-start.4 = (s32[43]{0:T(128)S(1)}, s32[43]{0:T(128)}, u32[]{:S(2)}) copy-start(s32[43]{0:T(128)} %param.8) | copy-start | bytes 520
  7.2 181.4 %all-gather.3.cloned.1.call-start = ((), (), s32[]{:S(2)}) async-start(), calls=%async_computation.9 | async-start | bytes 5570560 | tf_op jit(solution)/shard_map/all_gather | solution.py:58
  279.8 35.4 %all-to-all-start.4 = ((f32[64,1,1600]{2,1,0:T(1,128)}), f32[64,1,1600]{2,1,0:T(1,128)}, u32[]{:S(2)}, u32[]{:S(2)}) async-start(f32[64,1,1600]{2,1,0:T(1,128)} %reshape.76), calls=%async_computation.4 | async-start | bytes 851968 | tf_op jit(solution)/shard_map/all_to_all | solution.py:9
  290.3 211.6 %all-gather.5.cloned.1.call-start = ((), (), s32[]{:S(2)}) async-start(), calls=%async_computation.10 | async-start | bytes 5570560 | tf_op jit(solution)/shard_map/all_gather | solution.py:58
  331.9 175.1 %copy-start.2 = (f32[5,2048]{1,0:T(8,128)}, f32[5,2048]{1,0:T(8,128)S(1)}, u32[]{:S(2)}) copy-start(f32[5,2048]{1,0:T(8,128)S(1)} %fusion.20) | copy-start | bytes 122884
  524.5 44.5 %copy-start.1 = (f32[40,2048]{1,0:T(8,128)S(1)}, f32[40,2048]{1,0:T(8,128)}, u32[]{:S(2)}) copy-start(f32[40,2048]{1,0:T(8,128)} %reshape.50) | copy-start | bytes 983044
Sparse Core Ops, SparseCore 0:
  32.7 155.8 all-gather.2
  355.2 146.6 all-gather.4
where the time goes:
time: 606 us; the launch traced here: 604 us
  waiting for transfers between devices  327 us (54%)
  blocking collectives  171 us (28%)
  local copies, waits for them, and re-layouts  41.4 us (7%)
  other arithmetic  19.6 us (3%)
  matrix products  19.6 us (3%)
  between operations  14.3 us (2%)
  starting transfers between devices  10.7 us (2%)
    all_gather x2, waiting for transfers between devices, operator_apply(): panel = lax.all_gather(panel, 'row', axis=1, tiled=True)  303 us
    all_to_all x4, blocking collectives, copy_for_each(): lax.all_to_all(jnp.broadcast_to(shard[None], (devices, *shard.shape)), ax...  90.2 us
    all_to_all x4, blocking collectives, summed_on_arrival(): lax.all_to_all(parts, axis, split_axis=0, concat_axis=0, tiled=True)  81.2 us
    all_to_all x1, waiting for transfers between devices, copy_for_each(): lax.all_to_all(jnp.broadcast_to(shard[None], (devices, *shard.shape)), ax...  24.7 us
    dot_general x2, matrix products, block_product(): jnp.einsum('suv,ksv->ksu', tiles, picked, precision=lax.Precision.HIGHEST)  13.7 us
  transfers between devices with their start and end apart: 3, of which 3 were waited for; matrix products, arithmetic and copies ran while one was open for 0% of the time, Pallas kernels for 0%

commit v1 on v0

v1 whole, which is shorter than its diff:
```python
import jax
import jax.numpy as jnp
from jax import lax
from jax.experimental import pallas as pl
from jax.experimental.pallas import tpu as pltpu
from jax.sharding import PartitionSpec as P

MESH = pl.DeviceIdType.MESH
NZ = 16
NY = 4
NX = 4
NZL = 4
ROWS = 80
SLOTS = 43
PAD = 48
KALL = 40
OUT = 64
F32 = jnp.float32
BF16 = jnp.bfloat16


def split(v):
    hi = v.astype(BF16)
    lo = (v - hi.astype(F32)).astype(BF16)
    return hi, lo


def dot_nt(a, b):
    return lax.dot_general(a, b, (((1,), (1,)), ((), ())), preferred_element_type=F32)


def rem(a, n):
    return lax.rem(a, jnp.int32(n))


def div(a, n):
    return lax.div(a, jnp.int32(n))


def apply_kernel(
    x_ref, tiles_hbm, start_ref, local_ref, out_ref, whole_ref,
    tiles_v, panel, prods, y_ref, part, far, near, tail, gathered,
    tile_sem, send_sem, zr, zl_sem, yf, yh, d2d, core_s, core_r, x_s, x_r, q_s, q_r,
):
    row = lax.axis_index("row")
    x = lax.axis_index("col")
    cut = lax.axis_index("cuts")
    zh, y = div(row, NY), rem(row, NY)
    zlo, c = div(cut, 2), rem(cut, 2)
    z = zh * NZL + zlo

    def dev(zz, yy, xx, cc):
        return {"row": div(zz, NZL) * NY + yy, "col": xx, "cuts": rem(zz, NZL) * 2 + cc}

    right_z, left_z = rem(z + 1, NZ), rem(z + NZ - 1, NZ)
    up, down = rem(y + 1, NY), rem(y + NY - 1, NY)
    far_y = rem(y + 2, NY)
    xr, xl, xf = rem(x + 1, NX), rem(x + NX - 1, NX), rem(x + 2, NX)
    d_zr, d_zl = dev(right_z, y, x, c), dev(left_z, y, x, c)
    d_up, d_down = dev(z, up, x, c), dev(z, down, x, c)
    d_xr, d_xl = dev(z, y, xr, c), dev(z, y, xl, c)
    d_core = dev(z, y, x, 1 - c)
    d_q = [dev(zh * NZL + rem(zlo + d, NZL), y, x, c) for d in (1, 2, 3)]
    peers = [d_zr, d_zl, d_up, d_down, d_xr, d_xl, d_core] + d_q

    tile_copy = pltpu.make_async_copy(tiles_hbm, tiles_v, tile_sem)
    tile_copy.start()

    barrier = pltpu.get_barrier_semaphore()
    for p in peers:
        pl.semaphore_signal(barrier, inc=1, device_id=p, device_id_type=MESH)
    pl.semaphore_wait(barrier, len(peers))

    def block(zz, yy, cc, part_at=0, size=ROWS):
        index = (div(zz, NZL) * NY + yy) * 8 + rem(zz, NZL) * 2 + cc
        return panel.at[pl.ds(pl.multiple_of(index * ROWS + part_at, 8), size)]

    def copy(src, dst, s, r, d):
        return pltpu.make_async_remote_copy(
            src_ref=src, dst_ref=dst, send_sem=s, recv_sem=r, device_id=d, device_id_type=MESH
        )

    def zsrc(o):
        return rem(z + NZ - o, NZ)

    def emit(o):
        b = block(zsrc(o), y, c)
        src = x_ref if o == 0 else b
        copy(src, b, send_sem, yf.at[o], d_up).start()
        copy(src, b, send_sem, yf.at[NZ + o], d_down).start()
        copy(src, b, send_sem, d2d, d_core).start()

    def y_arrive(o):
        b = block(zsrc(o), down, c)
        copy(b, b, send_sem, yf.at[o], d_up).wait_recv()
        h = block(zsrc(o), down, c, 0, ROWS // 2)
        copy(h, h, send_sem, yh.at[o], d_up).start()
        copy(b, b, send_sem, d2d, d_core).start()
        b = block(zsrc(o), up, c)
        copy(b, b, send_sem, yf.at[NZ + o], d_down).wait_recv()
        h = block(zsrc(o), up, c, ROWS // 2, ROWS // 2)
        copy(h, h, send_sem, yh.at[NZ + o], d_down).start()
        copy(b, b, send_sem, d2d, d_core).start()

    def h_arrive(o):
        h = block(zsrc(o), far_y, c, 0, ROWS // 2)
        copy(h, h, send_sem, yh.at[o], d_up).wait_recv()
        h = block(zsrc(o), far_y, c, ROWS // 2, ROWS // 2)
        copy(h, h, send_sem, yh.at[NZ + o], d_down).wait_recv()
        b = block(zsrc(o), far_y, c)
        copy(b, b, send_sem, d2d, d_core).start()

    own = block(z, y, c)
    copy(x_ref, own, send_sem, zr.at[0], d_zr).start()
    copy(x_ref, own, send_sem, zl_sem.at[0], d_zl).start()
    emit(0)
    own[...] = x_ref[...]
    prods[...] = jnp.zeros_like(prods)
    before, older = [0], []
    for t in range(8):
        now = [t + 1]
        b = block(zsrc(t + 1), y, c)
        copy(b, b, send_sem, zr.at[t], d_zr).wait_recv()
        if t < 7:
            copy(b, b, send_sem, zr.at[t + 1], d_zr).start()
            b = block(zsrc(15 - t), y, c)
            copy(b, b, send_sem, zl_sem.at[t], d_zl).wait_recv()
            if t < 6:
                copy(b, b, send_sem, zl_sem.at[t + 1], d_zl).start()
            now.append(15 - t)
        for o in now:
            emit(o)
        for o in before:
            y_arrive(o)
        for o in older:
            h_arrive(o)
        before, older = now, before
    for o in before:
        y_arrive(o)
    for o in older + before:
        h_arrive(o)
    half = panel.at[pl.ds(0, 64 * ROWS)]
    copy(half, half, send_sem, d2d, d_core).wait_recv()
    most = panel.at[pl.ds(0, 127 * ROWS)]
    copy(most, most, send_sem, d2d, d_core).wait_send()

    tile_copy.wait()

    def slot(s):
        p_hi, p_lo = split(panel[pl.ds(start_ref[s], KALL, stride=16), :])
        t_hi, t_lo = split(tiles_v[s])
        prods[pl.ds(s, KALL, stride=PAD), :] = (
            dot_nt(p_hi, t_hi) + (dot_nt(p_lo, t_hi) + dot_nt(p_hi, t_lo))
        )

    def slots(i, carry):
        for j in range(7):
            slot(i * 7 + j)
        return carry

    lax.fori_loop(0, 6, slots, 0)
    slot(42)

    onehot = (
        lax.broadcasted_iota(jnp.int32, (OUT, 2 * PAD), 0) == local_ref[...]
    ).astype(F32).astype(BF16)

    half_rows = 20
    core_copies = []
    for q in range(NZL):
        for par in range(2):
            for kk in range(5):
                k = q * 10 + par * 5 + kk
                hi, lo = split(prods[pl.ds(k * PAD, PAD), :])
                y_ref[par, q * 5 + kk] = jnp.dot(
                    onehot, jnp.concatenate([hi, lo], axis=0), preferred_element_type=F32
                )
        cp = copy(
            y_ref.at[1 - c, pl.ds(q * 5, 5)], part.at[pl.ds(q * 5, 5)],
            core_s.at[q], core_r.at[q], d_core,
        )
        cp.start()
        core_copies.append(cp)

    total = y_ref.at[c]
    for q in range(NZL):
        core_copies[q].wait_recv()
        rows_q = pl.ds(q * 5, 5)
        total[rows_q] = total[rows_q] + part[rows_q]

    def seg(xx, first):
        return total.at[pl.ds(first, 10), pl.ds(pl.multiple_of(xx * 16, 16), 16)]

    far_r = copy(seg(xf, 0), far.at[0], x_s.at[0], x_r.at[0], d_xr)
    far_l = copy(seg(xf, 10), far.at[1], x_s.at[1], x_r.at[1], d_xl)
    near_rb = copy(seg(xr, 10), near.at[0, pl.ds(10, 10)], x_s.at[2], x_r.at[2], d_xr)
    near_la = copy(seg(xl, 0), near.at[1, pl.ds(0, 10)], x_s.at[3], x_r.at[3], d_xl)
    near_ra = copy(seg(xr, 0), near.at[0, pl.ds(0, 10)], x_s.at[4], x_r.at[4], d_xr)
    near_lb = copy(seg(xl, 10), near.at[1, pl.ds(10, 10)], x_s.at[5], x_r.at[5], d_xl)
    far_r.start()
    far_l.start()
    near_rb.start()
    near_la.start()
    far_r.wait_recv()
    seg(xr, 0)[...] = seg(xr, 0)[...] + far[0]
    near_ra.start()
    far_l.wait_recv()
    seg(xl, 10)[...] = seg(xl, 10)[...] + far[1]
    near_lb.start()
    near_la.wait_recv()
    near_ra.wait_recv()
    tail[pl.ds(0, 10)] = seg(x, 0)[...] + near[0, pl.ds(0, 10)] + near[1, pl.ds(0, 10)]
    near_rb.wait_recv()
    near_lb.wait_recv()
    tail[pl.ds(10, 10)] = seg(x, 10)[...] + near[0, pl.ds(10, 10)] + near[1, pl.ds(10, 10)]

    q_copies = []
    for d in (1, 2, 3):
        to = rem(zlo + d, NZL)
        cp = copy(
            tail.at[pl.ds(to * 5, 5)], gathered.at[d - 1], q_s.at[d - 1], q_r.at[d - 1], d_q[d - 1]
        )
        cp.start()
        q_copies.append(cp)
    whole_ref[...] = panel[pl.ds(pl.multiple_of(row * 8 * ROWS, 8), 8 * ROWS), :]
    acc = tail[pl.ds(zlo * 5, 5)]
    for cp in q_copies:
        cp.wait_recv()
    out_ref[...] = acc + gathered[0] + gathered[1] + gathered[2]

    for cp in core_copies + [far_r, far_l, near_rb, near_la, near_ra, near_lb] + q_copies:
        cp.wait_send()


def apply_call(vectors, tiles, start, local):
    dma = pltpu.SemaphoreType.DMA
    vmem = pl.BlockSpec(memory_space=pltpu.VMEM)
    return pl.pallas_call(
        apply_kernel,
        name="operator_apply",
        out_shape=(
            jax.ShapeDtypeStruct((5, 16, 128), F32),
            jax.ShapeDtypeStruct((8 * ROWS, 128), F32),
        ),
        in_specs=[
            vmem,
            pl.BlockSpec(memory_space=pl.ANY),
            pl.BlockSpec(memory_space=pltpu.SMEM),
            vmem,
        ],
        out_specs=(vmem, vmem),
        scratch_shapes=[
            pltpu.VMEM((SLOTS, 128, 128), F32),
            pltpu.VMEM((128 * ROWS, 128), F32),
            pltpu.VMEM((KALL * PAD, 128), F32),
            pltpu.VMEM((2, 20, OUT, 128), F32),
            pltpu.VMEM((20, OUT, 128), F32),
            pltpu.VMEM((2, 10, 16, 128), F32),
            pltpu.VMEM((2, 20, 16, 128), F32),
            pltpu.VMEM((20, 16, 128), F32),
            pltpu.VMEM((3, 5, 16, 128), F32),
            dma, dma, dma((8,)), dma((7,)), dma((32,)), dma((32,)), dma,
            dma((4,)), dma((4,)), dma((6,)), dma((6,)), dma((3,)), dma((3,)),
        ],
        compiler_params=pltpu.CompilerParams(collective_id=0, has_side_effects=True),
    )(vectors, tiles, start, local)


def hdot(a, b):
    return jnp.dot(a, b, precision=lax.Precision.HIGHEST, preferred_element_type=F32)


def shards(warm, tiles, tile_rows, tile_cols):
    items = 131072
    local = tile_rows - lax.axis_index("row") * OUT
    local = jnp.pad(local, (0, PAD - SLOTS), constant_values=-1)
    local = jnp.concatenate([local, local]).reshape(1, 2 * PAD)
    start = tile_cols // 64 * (8 * ROWS) + tile_cols % 16
    image, _ = apply_call(warm.reshape(ROWS, 128), tiles, start, local)
    product, whole = apply_call(image.reshape(ROWS, 128), tiles, start, local)
    whole = whole.reshape(KALL, 2048)
    product = lax.all_gather(product.reshape(5, 2048), "cuts", axis=0, tiled=True)
    sums = jnp.concatenate([hdot(whole, whole.T), hdot(whole, product.T)], axis=1)
    sums = lax.psum(sums, ("row", "col")) / items
    gram, mixed = sums[:, :KALL], sums[:, KALL:]
    lower = jnp.linalg.cholesky(gram)
    inverse = lax.linalg.triangular_solve(
        lower, jnp.eye(KALL, dtype=F32), left_side=True, lower=True
    )
    projected = hdot(inverse, hdot(mixed, inverse.T))
    mine = lax.dynamic_slice_in_dim(inverse, lax.axis_index("cuts") * 5, 5, 0)
    basis = hdot(mine, whole)
    columns = lax.dynamic_slice_in_dim(projected, lax.axis_index("cuts") * 5, 5, 1)
    residual = hdot(mine, product) - hdot(hdot(columns.T, inverse), whole)
    return (basis, residual)


def solution(mesh):
    return jax.shard_map(
        shards,
        mesh=mesh,
        in_specs=(
            P("cuts", ("row", "col")),
            P(("row", "col", "cuts"), None, None),
            P(("row", "col", "cuts")),
            P(("row", "col", "cuts")),
        ),
        out_specs=(P("cuts", ("row", "col")), P("cuts", ("row", "col"))),
        check_vma=False,
    )
```

time: 606 us -> 593 us (0.979)
  the two profiles are of different devices: /device:TPU:1 before, /device:TPU:32 now
where the time goes in v1:
time: 593 us
  blocking collectives  450 us (76%)
  Pallas kernels  124 us (21%)
  other arithmetic  10.6 us (2%)
    psum x1, blocking collectives, shards(): sums = lax.psum(sums, ('row', 'col')) / items  435 us
    pallas_call x2, Pallas kernels, apply_call(): pl.pallas_call(apply_kernel, name='operator_apply', out_shape=(jax.ShapeD...  124 us
    all_gather x1, blocking collectives, shards(): lax.all_gather(product.reshape(5, 2048), 'cuts', axis=0, tiled=True)  14.8 us

profile of v1, /device:TPU:32, one launch (start us, length us, event | category | flops | bytes accessed | tf_op | source)
XLA Modules:
  0.0 592.7 jit_solution(9595410293989377161)
XLA Ops:
  0.6 0.7 broadcast_subtract_fusion
  1.3 0.7 add_bitcast_fusion.local_ref
  2.0 1.2 fusion.12.start_ref
  3.1 1.5 reshape.28.x_ref
  4.6 66.0 %operator_apply.2 = (f32[5,16,128]{2,1,0:T(8,128)}, f32[640,128]{1,0:T(8,128)}) custom-call(f32[80,128]{1,0:T(8,128)} %reshape.28.x_ref, f32[43,128,128]{2,1,0:T(8,128)} %tiles_hbm.3, s32[43]{0:T(128)} %fusion.12.start_ref, s32[1,96]{1,0:T(1,128)} %add_bitcast_fusion.local_ref), custom_call_target="tpu_custom_call" | custom-call | tf_op jit(solution)/shard_map/operator_apply/pallas_call | solution.py:238
  70.6 58.2 %operator_apply.3 = (f32[5,16,128]{2,1,0:T(8,128)}, f32[640,128]{1,0:T(8,128)}) custom-call(f32[80,128]{1,0:T(8,128)} %bitcast.24, f32[43,128,128]{2,1,0:T(8,128)} %tiles_hbm.3, s32[43]{0:T(128)} %fusion.12.start_ref, s32[1,96]{1,0:T(1,128)} %add_bitcast_fusion.local_ref), custom_call_target="tpu_custom_call" | custom-call | tf_op jit(solution)/shard_map/operator_apply/pallas_call | solution.py:238
  128.8 1.0 reshape.31
  129.9 0.8 reshape.33
  130.6 14.8 %all-gather = f32[8,5,2048]{2,1,0:T(8,128)S(1)} all-gather(f32[1,5,2048]{2,1,0:T(8,128)S(1)} %reshape.33), channel_id=1, replica_groups=mesh['row'=16,'col'=4,'cuts'=8] {'cuts'}, dimensions={0}, use_global_device_ids=true | all-gather | bytes 368640 | tf_op jit(solution)/shard_map/all_gather | solution.py:282
  145.4 0.1 reshape.34
  145.5 0.4 fusion.17
  145.9 0.4 fusion.16
  146.3 435.3 %psum.7 = f32[40,80]{0,1:T(8,128)S(1)} all-reduce(f32[40,80]{0,1:T(8,128)S(1)} %pad_maximum_fusion), channel_id=1, replica_groups=mesh['row'=16,'col'=4,'cuts'=8] {'row','col'}, use_global_device_ids=true, to_apply=%region_0.1 | all-reduce | flops 3200 | bytes 25600 | tf_op jit(solution)/shard_map/psum | solution.py:284
  581.6 0.1 copy.14
  581.7 3.6 cholesky.17
  585.4 0.6 compare_reduce_fusion
  586.0 0.7 fusion
  586.7 3.1 custom-call.6
  589.8 0.2 fusion.3
  590.0 0.2 fusion.1
  590.2 0.2 fusion.18
  590.5 0.1 fusion.6
  590.6 0.3 fusion.8
  590.9 0.9 convolution_subtract_fusion
  591.8 0.9 fusion.10
  (6 shorter events, 0.1 us)

commit v2 on v0

v2 whole, which is shorter than its diff:
```python
import jax
import jax.numpy as jnp
from jax import lax
from jax.experimental import pallas as pl
from jax.experimental.pallas import tpu as pltpu
from jax.sharding import PartitionSpec as P

MESH = pl.DeviceIdType.MESH
NZ = 16
NY = 4
NX = 4
NZL = 4
ROWS = 80
SLOTS = 43
PAD = 48
KALL = 40
KLOC = 5
OUT = 64
ITEMS = 131072
F32 = jnp.float32
BF16 = jnp.bfloat16


def split(v):
    hi = v.astype(BF16)
    lo = (v - hi.astype(F32)).astype(BF16)
    return hi, lo


def dot_nt(a, b):
    return lax.dot_general(a, b, (((1,), (1,)), ((), ())), preferred_element_type=F32)


def exact_nt(a, b):
    return lax.dot_general(
        a, b, (((1,), (1,)), ((), ())),
        precision=lax.Precision.HIGHEST, preferred_element_type=F32,
    )


def exact(a, b):
    return jnp.dot(a, b, precision=lax.Precision.HIGHEST, preferred_element_type=F32)


def rem(a, n):
    return lax.rem(a, jnp.int32(n))


def div(a, n):
    return lax.div(a, jnp.int32(n))


def inverse_factor(gram):
    row = lax.broadcasted_iota(jnp.int32, (KALL, 128), 0)
    lane = lax.broadcasted_iota(jnp.int32, (KALL, 128), 1)
    m = jnp.where(lane < KALL, gram, 0.0) + (lane == row + 64).astype(F32)
    for j in range(KALL):
        d = m[j : j + 1, j : j + 1]
        r0 = lax.rsqrt(d)
        scale = r0 * (1.5 - 0.5 * d * r0 * r0)
        pivot = m[j : j + 1, :] * scale
        column = m[:, j : j + 1] * scale
        m = jnp.where(row > j, m - column * pivot, jnp.where(row == j, pivot, m))
    return m[:, 64 : 64 + KALL]


def kernel(
    x_ref, tiles_hbm, start_ref, local_ref, basis_ref, residual_ref,
    tiles_v, panel_a, panel_b, prods, y_ref, part, far, near, tail, mixed, gathered, total_u, image,
    product, basis_all, gsum, psum, tile_sem, ag_send, zr_s, zl_s, yf, yh, d2d,
    core_s, core_r, x_s, x_r, q_s, q_r, w_s, w_r, g_s, g_r, p_s, p_r,
):
    row = lax.axis_index("row")
    x = lax.axis_index("col")
    cut = lax.axis_index("cuts")
    zh, y = div(row, NY), rem(row, NY)
    zlo, c = div(cut, 2), rem(cut, 2)
    z = zh * NZL + zlo

    def dev(zz, yy, xx, cc):
        return {"row": div(zz, NZL) * NY + yy, "col": xx, "cuts": rem(zz, NZL) * 2 + cc}

    up, down, far_y = rem(y + 1, NY), rem(y + NY - 1, NY), rem(y + 2, NY)
    xr, xl, xf = rem(x + 1, NX), rem(x + NX - 1, NX), rem(x + 2, NX)
    d_zr, d_zl = dev(rem(z + 1, NZ), y, x, c), dev(rem(z + NZ - 1, NZ), y, x, c)
    d_x = [dev(z, y, rem(x + d, NX), c) for d in (1, 2, 3)]
    d_y = [dev(z, rem(y + d, NY), x, c) for d in (1, 2, 3)]
    d_up, d_down, d_xr, d_xl = d_y[0], d_y[2], d_x[0], d_x[2]
    d_core = dev(z, y, x, 1 - c)
    d_q = [dev(zh * NZL + rem(zlo + d, NZL), y, x, c) for d in (1, 2, 3)]
    d_h = [dev(rem(zh + d, 4) * NZL + zlo, y, x, c) for d in (1, 2, 3)]
    peers = [d_zr, d_zl, d_core] + d_x + d_y + d_q + d_h

    tile_copy = pltpu.make_async_copy(tiles_hbm, tiles_v, tile_sem)
    tile_copy.start()

    barrier = pltpu.get_barrier_semaphore()
    for p in peers:
        pl.semaphore_signal(barrier, inc=1, device_id=p, device_id_type=MESH)
    pl.semaphore_wait(barrier, len(peers))

    def copy(src, dst, s, r, d):
        return pltpu.make_async_remote_copy(
            src_ref=src, dst_ref=dst, send_sem=s, recv_sem=r, device_id=d, device_id_type=MESH
        )

    def zsrc(o):
        return rem(z + NZ - o, NZ)

    def gather(n, x_ref, panel, after_z):
        send_sem = ag_send.at[n]

        def block(zz, yy, part_at=0, size=ROWS):
            index = (div(zz, NZL) * NY + yy) * 8 + rem(zz, NZL) * 2 + c
            return panel.at[pl.ds(pl.multiple_of(index * ROWS + part_at, 8), size)]

        def emit(o):
            b = block(zsrc(o), y)
            src = x_ref if o == 0 else b
            copy(src, b, send_sem, yf.at[n, o], d_up).start()
            copy(src, b, send_sem, yf.at[n, NZ + o], d_down).start()
            copy(src, b, send_sem, d2d.at[n, 0], d_core).start()

        def y_arrive(o):
            for at, side, d in ((0, down, d_up), (1, up, d_down)):
                b = block(zsrc(o), side)
                copy(b, b, send_sem, yf.at[n, at * NZ + o], d).wait_recv()
                h = block(zsrc(o), side, at * (ROWS // 2), ROWS // 2)
                copy(h, h, send_sem, yh.at[n, at * NZ + o], d).start()
                copy(b, b, send_sem, d2d.at[n, 1], d_core).start()

        def h_arrive(o):
            for at, d in ((0, d_up), (1, d_down)):
                h = block(zsrc(o), far_y, at * (ROWS // 2), ROWS // 2)
                copy(h, h, send_sem, yh.at[n, at * NZ + o], d).wait_recv()
            b = block(zsrc(o), far_y)
            copy(b, b, send_sem, d2d.at[n, 1], d_core).start()

        own = block(z, y)
        copy(x_ref, own, send_sem, zr_s.at[n, 0], d_zr).start()
        copy(x_ref, own, send_sem, zl_s.at[n, 0], d_zl).start()
        emit(0)
        own[...] = x_ref[...]
        before, older = [0], []
        for t in range(8):
            now = [t + 1]
            b = block(zsrc(t + 1), y)
            copy(b, b, send_sem, zr_s.at[n, t], d_zr).wait_recv()
            if t < 7:
                copy(b, b, send_sem, zr_s.at[n, t + 1], d_zr).start()
                b = block(zsrc(15 - t), y)
                copy(b, b, send_sem, zl_s.at[n, t], d_zl).wait_recv()
                if t < 6:
                    copy(b, b, send_sem, zl_s.at[n, t + 1], d_zl).start()
                now.append(15 - t)
            for o in now:
                emit(o)
            for o in before:
                y_arrive(o)
            for o in older:
                h_arrive(o)
            before, older = now, before
        some = panel.at[pl.ds(0, 16 * ROWS)]
        copy(some, some, send_sem, d2d.at[n, 0], d_core).wait_recv()
        after_z()
        for o in before:
            y_arrive(o)
        for o in older + before:
            h_arrive(o)
        some = panel.at[pl.ds(0, 48 * ROWS)]
        copy(some, some, send_sem, d2d.at[n, 1], d_core).wait_recv()

    def gather_done(n, panel):
        most = panel.at[pl.ds(0, 127 * ROWS)]
        copy(most, most, ag_send.at[n], d2d.at[n, 0], d_core).wait_send()

    def exchange(buf, sems, stage, at, devices, value):
        buf[stage, at] = value
        cps = []
        for i, d in enumerate(devices):
            k = stage * 3 + i
            cp = copy(buf.at[stage, at], buf.at[stage, at], sems[0].at[k], sems[1].at[k], d)
            cp.start()
            cps.append(cp)
        return cps

    def exchanged(buf, stage, cps):
        for cp in cps:
            cp.wait_recv()
        return (buf[stage, 0] + buf[stage, 1]) + (buf[stage, 2] + buf[stage, 3])

    def products(panel):
        def slot(s):
            p_hi, p_lo = split(panel[pl.ds(start_ref[s], KALL, stride=16), :])
            t_hi, t_lo = split(tiles_v[s])
            prods[pl.ds(s, KALL, stride=PAD), :] = (
                dot_nt(p_hi, t_hi) + (dot_nt(p_lo, t_hi) + dot_nt(p_hi, t_lo))
            )

        def slots(i, carry):
            for j in range(7):
                slot(i * 7 + j)
            return carry

        lax.fori_loop(0, 6, slots, 0)
        slot(42)

    def reduce_scatter(n, between, after_x, beside, result):
        onehot = (
            lax.broadcasted_iota(jnp.int32, (OUT, 2 * PAD), 0) == local_ref[...]
        ).astype(F32).astype(BF16)
        pending = []
        for q in range(4):
            for kk in range(10):
                k = q * 10 + kk
                hi, lo = split(prods[pl.ds(k * PAD, PAD), :])
                summed = jnp.dot(
                    onehot, jnp.concatenate([hi, lo], axis=0), preferred_element_type=F32
                )
                y_ref[0, k] = summed[: OUT // 2]
                y_ref[1, k] = summed[OUT // 2 :]
            rows_q = pl.ds(q * 10, 10)
            cp = copy(
                y_ref.at[1 - c, rows_q], part.at[n, rows_q], core_s.at[n, q], core_r.at[n, q], d_core
            )
            cp.start()
            pending.append(cp)
        total = y_ref.at[c]
        for q in range(4):
            pending[q].wait_recv()
            rows_q = pl.ds(q * 10, 10)
            total[rows_q] = total[rows_q] + part[n, rows_q]

        def seg(xx, first):
            return total.at[pl.ds(first, 20), pl.ds(pl.multiple_of(xx * 8, 8), 8)]

        lo_half, hi_half = pl.ds(0, 20), pl.ds(20, 20)
        xs, xv = x_s.at[n], x_r.at[n]
        far_r = copy(seg(xf, 0), far.at[n, 0], xs.at[0], xv.at[0], d_xr)
        far_l = copy(seg(xf, 20), far.at[n, 1], xs.at[1], xv.at[1], d_xl)
        near_rb = copy(seg(xr, 20), near.at[n, 0, hi_half], xs.at[2], xv.at[2], d_xr)
        near_la = copy(seg(xl, 0), near.at[n, 1, lo_half], xs.at[3], xv.at[3], d_xl)
        near_ra = copy(seg(xr, 0), near.at[n, 0, lo_half], xs.at[4], xv.at[4], d_xr)
        near_lb = copy(seg(xl, 20), near.at[n, 1, hi_half], xs.at[5], xv.at[5], d_xl)
        pending += [far_r, far_l, near_rb, near_la, near_ra, near_lb]
        far_r.start()
        far_l.start()
        near_rb.start()
        near_la.start()
        between()
        far_r.wait_recv()
        seg(xr, 0)[...] = seg(xr, 0)[...] + far[n, 0]
        near_ra.start()
        far_l.wait_recv()
        seg(xl, 20)[...] = seg(xl, 20)[...] + far[n, 1]
        near_lb.start()
        near_la.wait_recv()
        near_ra.wait_recv()
        low = seg(x, 0)[...] + near[n, 0, lo_half] + near[n, 1, lo_half]
        tail[pl.ds(0, 160)] = low.reshape(160, 128)
        near_rb.wait_recv()
        near_lb.wait_recv()
        high = seg(x, 20)[...] + near[n, 0, hi_half] + near[n, 1, hi_half]
        tail[pl.ds(160, 160)] = high.reshape(160, 128)
        after_x()

        sends = []
        for d in (1, 2, 3):
            to = rem(zlo + d, NZL)
            cp = copy(
                mixed.at[n, pl.ds(pl.multiple_of(to * ROWS, 8), ROWS)], gathered.at[n, d - 1],
                q_s.at[n, d - 1], q_r.at[n, d - 1], d_q[d - 1],
            )
            cp.start()
            sends.append(cp)
        beside()
        for cp in sends:
            cp.wait_recv()
        total_u[n] = (
            mixed[n, pl.ds(pl.multiple_of(zlo * ROWS, 8), ROWS)]
            + gathered[n, 0] + gathered[n, 1] + gathered[n, 2]
        )
        swaps = []
        for k in range(KLOC):
            mine = pl.ds(pl.multiple_of((c * KLOC + k) * 8, 8), 8)
            theirs = pl.ds(pl.multiple_of(((1 - c) * KLOC + k) * 8, 8), 8)
            here = pl.ds(pl.multiple_of(k * 16 + c * 8, 8), 8)
            cp = copy(
                total_u.at[n, theirs], result.at[here], w_s.at[n, k], w_r.at[n, k], d_core
            )
            cp.start()
            swaps.append(cp)
            result[here] = total_u[n, mine]
        for cp in swaps:
            cp.wait_recv()
        return pending + sends + swaps

    def nothing():
        pass

    def plain_tail():
        mixed[0] = tail[...]

    prods[...] = jnp.zeros_like(prods)
    gather(0, x_ref, panel_a, nothing)
    tile_copy.wait()
    products(panel_a)
    sent = reduce_scatter(0, nothing, plain_tail, nothing, image)
    for cp in sent:
        cp.wait_send()

    first = pl.multiple_of(row * 8 * ROWS, 8)
    state = {}

    def whole(b):
        return panel_b[pl.ds(first + b, KALL, stride=16), :]

    def wide(v):
        return jnp.concatenate([v, jnp.zeros((v.shape[0], 128 - v.shape[1]), F32)], axis=1)

    def gram_start():
        gram = jnp.zeros((KALL, KALL), F32)
        for b in range(16):
            v = whole(b)
            gram = gram + exact_nt(v, v)
        state["x"] = exchange(gsum, (g_s, g_r), 0, x, d_x, wide(gram))

    gather(1, image, panel_b, gram_start)
    state["y"] = exchange(gsum, (g_s, g_r), 1, y, d_y, exchanged(gsum, 0, state["x"]))
    products(panel_b)
    state["h"] = exchange(gsum, (g_s, g_r), 2, zh, d_h, exchanged(gsum, 1, state["y"]))

    def factor():
        state["inverse"] = inverse_factor(exchanged(gsum, 2, state["h"]) * (1.0 / ITEMS))

    def mix_tail():
        for j in range(8):
            at = pl.ds(j, KALL, stride=8)
            mixed[1, at, :] = exact(state["inverse"], tail[at, :])

    def write_basis():
        for b in range(16):
            basis_all[pl.ds(b, KALL, stride=16), :] = exact(state["inverse"], whole(b))
        basis_ref[...] = basis_all[pl.ds(pl.multiple_of(cut * ROWS, 8), ROWS), :]

    sent = reduce_scatter(1, factor, mix_tail, write_basis, product)

    local = jnp.zeros((KLOC, KALL), F32)
    for b in range(16):
        local = local + exact_nt(
            product[pl.ds(b, KLOC, stride=16), :], basis_all[pl.ds(b, KALL, stride=16), :]
        )
    local = jnp.concatenate([wide(local), jnp.zeros((3, 128), F32)], axis=0)
    p_sems = (p_s, p_r)
    px = exchange(psum, p_sems, 0, x, d_x, local)
    py = exchange(psum, p_sems, 1, y, d_y, exchanged(psum, 0, px))
    ph = exchange(psum, p_sems, 2, zh, d_h, exchanged(psum, 1, py))
    projected = exchanged(psum, 2, ph)[:KLOC, :KALL] * (1.0 / ITEMS)
    for b in range(16):
        at = pl.ds(b, KLOC, stride=16)
        residual_ref[at, :] = product[at, :] - exact(
            projected, basis_all[pl.ds(b, KALL, stride=16), :]
        )

    for cp in sent + state["x"] + state["y"] + state["h"] + px + py + ph:
        cp.wait_send()
    gather_done(0, panel_a)
    gather_done(1, panel_b)


def shards(warm, tiles, tile_rows, tile_cols):
    local = tile_rows - lax.axis_index("row") * OUT
    local = jnp.where(
        local >= 0, local % 16 // 8 * 32 + local // 16 * 8 + local % 8, -1
    )
    local = jnp.pad(local, (0, PAD - SLOTS), constant_values=-1)
    local = jnp.concatenate([local, local]).reshape(1, 2 * PAD)
    start = tile_cols // 64 * (8 * ROWS) + tile_cols % 16
    dma = pltpu.SemaphoreType.DMA
    vmem = pl.BlockSpec(memory_space=pltpu.VMEM)
    basis, residual = pl.pallas_call(
        kernel,
        name="operator_steps",
        out_shape=(jax.ShapeDtypeStruct((ROWS, 128), F32),) * 2,
        in_specs=[
            vmem,
            pl.BlockSpec(memory_space=pl.ANY),
            pl.BlockSpec(memory_space=pltpu.SMEM),
            vmem,
        ],
        out_specs=(vmem, vmem),
        scratch_shapes=[
            pltpu.VMEM((SLOTS, 128, 128), F32),
            pltpu.VMEM((128 * ROWS, 128), F32),
            pltpu.VMEM((128 * ROWS, 128), F32),
            pltpu.VMEM((KALL * PAD, 128), F32),
            pltpu.VMEM((2, KALL, OUT // 2, 128), F32),
            pltpu.VMEM((2, KALL, OUT // 2, 128), F32),
            pltpu.VMEM((2, 2, 20, 8, 128), F32),
            pltpu.VMEM((2, 2, KALL, 8, 128), F32),
            pltpu.VMEM((KALL * 8, 128), F32),
            pltpu.VMEM((2, KALL * 8, 128), F32),
            pltpu.VMEM((2, 3, ROWS, 128), F32),
            pltpu.VMEM((2, ROWS, 128), F32),
            pltpu.VMEM((ROWS, 128), F32),
            pltpu.VMEM((ROWS, 128), F32),
            pltpu.VMEM((KALL * 16, 128), F32),
            pltpu.VMEM((3, 4, KALL, 128), F32),
            pltpu.VMEM((3, 4, 8, 128), F32),
            dma, dma((2,)), dma((2, 8)), dma((2, 7)), dma((2, 32)), dma((2, 32)), dma((2, 2)),
            dma((2, 4)), dma((2, 4)), dma((2, 6)), dma((2, 6)), dma((2, 3)), dma((2, 3)),
            dma((2, 5)), dma((2, 5)), dma((9,)), dma((9,)), dma((9,)), dma((9,)),
        ],
        compiler_params=pltpu.CompilerParams(collective_id=0, has_side_effects=True),
    )(warm.reshape(ROWS, 128), tiles, start, local)
    return basis.reshape(KLOC, 2048), residual.reshape(KLOC, 2048)


def solution(mesh):
    return jax.shard_map(
        shards,
        mesh=mesh,
        in_specs=(
            P("cuts", ("row", "col")),
            P(("row", "col", "cuts"), None, None),
            P(("row", "col", "cuts")),
            P(("row", "col", "cuts")),
        ),
        out_specs=(P("cuts", ("row", "col")), P("cuts", ("row", "col"))),
        check_vma=False,
    )
```

time: 606 us -> 156 us (0.26)
  waiting for transfers between devices: 327 us -> 0 us
  blocking collectives: 171 us -> 0 us
  Pallas kernels: 0 us -> 148 us
  local copies, waits for them, and re-layouts: 41.4 us -> 4.31 us
  matrix products: 19.6 us -> 0 us
  other arithmetic: 19.6 us -> 2.52 us
  between operations: 14.3 us -> 0.65 us
  starting transfers between devices: 10.7 us -> 0 us
    all_gather x2 -> x0, waiting for transfers between devices: 303 us -> none  [operator_apply(): panel = lax.all_gather(panel, 'row', axis=1, tiled=True)]
    all_to_all x8 -> x0, blocking collectives: 171 us -> none  [the longest x4 90.2 us: copy_for_each(): lax.all_to_all(jnp.broadcast_to(shard[None], (devices, *shard.shape)), ax...]
    pallas_call x0 -> x1, Pallas kernels: none -> 148 us  [shards(): pl.pallas_call(kernel, name='operator_steps', out_shape=(jax.ShapeDtypeSt...]
    all_to_all x1 -> x0, waiting for transfers between devices: 24.7 us -> none  [copy_for_each(): lax.all_to_all(jnp.broadcast_to(shard[None], (devices, *shard.shape)), ax...]
    dot_general x8 -> x0, matrix products: 19.4 us -> none  [the longest x2 13.7 us: block_product(): jnp.einsum('suv,ksv->ksu', tiles, picked, precision=lax.Precision.HIGHEST)]
    reshape x7 -> x3, local copies, waits for them, and re-layouts: 14.9 us -> 4.3 us  [the longest x2 2.83 us: shards(): return (basis.reshape(KLOC, 2048), residual.reshape(KLOC, 2048))]
    all_to_all x1 -> x0, starting transfers between devices: 10.5 us -> none  [copy_for_each(): lax.all_to_all(jnp.broadcast_to(shard[None], (devices, *shard.shape)), ax...]
    another operation x4 -> x0, local copies, waits for them, and re-layouts: 9.47 us -> none  [in_blocks(): shard.reshape(*dims[:dim], devices, dims[dim] // devices, *dims[dim + 1:])]
  transfers between devices with their start and end apart: 3 -> 0, of which waited for: 3 -> 0; matrix products, arithmetic and copies ran while one was open for 0% -> 0% of each run, Pallas kernels for 0% -> 0%
where the time goes in v2:
time: 156 us
  Pallas kernels  148 us (95%)
  local copies, waits for them, and re-layouts  4.31 us (3%)
  other arithmetic  2.52 us (2%)
    pallas_call x1, Pallas kernels, shards(): pl.pallas_call(kernel, name='operator_steps', out_shape=(jax.ShapeDtypeSt...  148 us

profile of v2, /device:TPU:1, one launch (start us, length us, event | category | flops | bytes accessed | tf_op | source)
XLA Modules:
  0.0 155.6 jit_solution(1674272544366603886)
XLA Ops:
  0.6 0.7 compare_select_fusion
  1.3 0.7 add_bitcast_fusion.local_ref
  2.0 1.2 fusion.start_ref
  3.2 1.5 reshape.16.x_ref
  4.6 148.1 %operator_steps.1 = (f32[80,128]{1,0:T(8,128)}, f32[80,128]{1,0:T(8,128)}) custom-call(f32[80,128]{1,0:T(8,128)} %reshape.16.x_ref, f32[43,128,128]{2,1,0:T(8,128)} %tiles_hbm.1, s32[43]{0:T(128)} %fusion.start_ref, s32[1,96]{1,0:T(1,128)} %add_bitcast_fusion.local_ref), custom_call_target="tpu_custom_call" | custom-call | tf_op jit(solution)/shard_map/operator_steps/pallas_call | solution.py:381
  152.7 1.4 reshape.18
  154.2 1.4 reshape.19
  (1 shorter events, 0.0 us)
